TPU v7x, 256 devices: a whole 4x4x8 slice. The times are simulated.
256 devices in a mesh: row: 16 (over y, z_lo, core), col: 16 (over x, z_hi).
Axes of the slice: x: 4, y: 4, z: 8 (z_hi: 4, z_lo: 2; z = z_hi * 2 + z_lo), core: 2. Of those that a mesh axis runs over, the one named last changes fastest.
Arguments:
- start_field: float32 [1, 2, 4096, 8192], P(None, None, 'col', 'row'), may hold values from -6 to 6
- section_field: float32 [1, 2, 4096, 8192], P(None, None, 'col', 'row'), may hold values from -26 to 26
- start_term: float32 [1, 2, 4096, 8192], P(None, None, 'col', 'row'), may hold values from -6 to 6
- first_term: float32 [1, 2, 4096, 8192], P(None, None, 'col', 'row'), may hold values from -6 to 6
- second_term: float32 [1, 2, 4096, 8192], P(None, None, 'col', 'row'), may hold values from -6 to 6
Outputs:
- next_field: float32 [1, 2, 4096, 8192], P(None, None, 'col', 'row')
All inputs are finite; a program needn't handle non-finite values.
Results may differ from a plain program's by a relative error of at most 0.0001.
Values sent between devices are 32-bit elements; how exact they have to be, the bound alone decides.
A program may use at most 128 MiB of HBM per device.

v0:
```python
import functools
import math

import jax
import jax.numpy as jnp
import ml_dtypes
import numpy as np
from jax import lax
from jax.experimental import pallas as pl
from jax.experimental.pallas import tpu as pltpu
from jax.sharding import PartitionSpec as P

LENGTH = 8192
ROWS = 16
COLS = 16
DEVICES = ROWS * COLS
BLOCK_X = 256
BLOCK_Y = 512
LINES = 11
KEPT = 12
PAIRS = 33

viscous_rate = 1.5
wave_scale = 3.0
series_terms = 12

HIGH = jnp.bfloat16
FULL = jnp.float32


def section_weights(wave_x, wave_y):
    square = wave_x * wave_x + wave_y * wave_y
    kappa_x = wave_scale * wave_x.astype(FULL) / LENGTH
    kappa_y = wave_scale * wave_y.astype(FULL) / LENGTH
    kappa_sq = kappa_x * kappa_x + kappa_y * kappa_y
    zvalue = -viscous_rate * kappa_sq
    damping = jnp.exp(zvalue)
    near_zero = 27 * square < 2 * LENGTH * LENGTH

    def series(degree):
        running = jnp.full_like(zvalue, 1.0 / math.factorial(series_terms - 1 + degree))
        for term_index in range(series_terms - 2, -1, -1):
            running = running * zvalue + 1.0 / math.factorial(term_index + degree)
        return running

    clamped = jnp.where(near_zero, -1.0, zvalue)
    exp_clamped = jnp.exp(clamped)
    closed_one = (exp_clamped - 1.0) / clamped
    closed_two = (exp_clamped - 1.0 - clamped) / (clamped * clamped)
    closed_three = (exp_clamped - 1.0 - clamped - 0.5 * clamped * clamped) / (
        clamped * clamped * clamped
    )
    phi_one = jnp.where(near_zero, series(1), closed_one)
    phi_two = jnp.where(near_zero, series(2), closed_two)
    phi_three = jnp.where(near_zero, series(3), closed_three)
    weight_a = phi_one - 3.0 * phi_two + 4.0 * phi_three
    weight_b = phi_two - 2.0 * phi_three
    weight_c = 4.0 * phi_three - phi_two
    return damping, weight_a, weight_b, weight_c


def halves(table):
    table = np.asarray(table, np.float32)
    high = table.astype(ml_dtypes.bfloat16)
    low = (table - high.astype(np.float32)).astype(ml_dtypes.bfloat16)
    return np.stack([high, low])


@functools.lru_cache(None)
def tables():
    row = np.arange(KEPT * 8)
    kept_row = row // 8
    source_row = np.where(kept_row < KEPT // 2, kept_row, kept_row + ROWS - KEPT)
    part = row % 8 // 4
    index_a = 4 * source_row + row % 4
    index_c = np.arange(64)
    angle = 2 * np.pi / 64 * (index_c[:, None] * index_a[None, :] % 64)
    cosine, sine = np.cos(angle), np.sin(angle)
    real_rows = np.where(part == 0, -sine, -cosine)
    imag_rows = np.where(part == 0, cosine, -sine)
    first = np.concatenate([real_rows, imag_rows])
    real_out = np.where(part == 0, cosine, -sine)
    imag_out = np.where(part == 0, sine, cosine)
    last = np.concatenate([real_out, imag_out]).T
    index_b = np.arange(128)
    turn = 2 * np.pi / LENGTH * (index_c[:, None] * index_b[None, :])
    turns = np.stack([np.cos(turn), np.sin(turn)]).astype(np.float32)
    angle = 2 * np.pi / 128 * (index_b[:, None] * index_b[None, :] % 128)
    cosine, sine = np.cos(angle), np.sin(angle)
    second = np.zeros((2, 2, 128, 4, 2, 2, 32))
    for field in range(2):
        second[0, field, :, :, 0, field] = cosine.reshape(128, 4, 32)
        second[0, field, :, :, 1, field] = sine.reshape(128, 4, 32)
        second[1, field, :, :, 0, field] = -sine.reshape(128, 4, 32)
        second[1, field, :, :, 1, field] = cosine.reshape(128, 4, 32)
    second = second.reshape(512, 512)
    spin = 2 * np.pi / LENGTH * np.broadcast_to(index_b[None, :], (128, 128))
    base = np.stack(
        [cosine, -sine, np.cos(spin), -np.sin(spin), np.cos(spin.T), -np.sin(spin.T)]
    ).astype(np.float32)
    return halves(first), halves(second), halves(second.T), halves(last), turns, base


def split(values):
    high = values.astype(HIGH)
    return high, (values - high.astype(FULL)).astype(HIGH)


def times(left_high, left_low, right_high, right_low):
    dot = functools.partial(jnp.dot, preferred_element_type=FULL)
    return (
        dot(left_high, right_low) + dot(left_low, right_high)
    ) + dot(left_high, right_high)


def turned(values, upper):
    moved = pltpu.roll(values, 64, 1)
    return jnp.where(upper, moved, -moved)


def cosine_of(step, period):
    return math.cos(2 * math.pi * (step % period) / period)


def sine_of(step, period):
    return math.sin(2 * math.pi * (step % period) / period)


def scaled(factor, value):
    if abs(factor) < 1e-12:
        return None
    if abs(factor - 1) < 1e-12:
        return value
    if abs(factor + 1) < 1e-12:
        return -value
    return factor * value


def total(values):
    values = [value for value in values if value is not None]
    if not values:
        return None
    return functools.reduce(lambda a, b: a + b, values)


def plus(a, b):
    return b if a is None else a if b is None else a + b


def minus(a, b):
    return a if b is None else -b if a is None else a - b


def spread_lines(lines, upper):
    turns = [turned(line, upper) for line in lines]
    out = [None] * 32
    for step in range(9):
        sums = []
        for parity in range(2):
            picked = range(parity, LINES, 2)
            sums.append(total(scaled(cosine_of(l * step, 32), lines[l]) for l in picked))
            sums.append(total(scaled(sine_of(l * step, 32), turns[l]) for l in picked))
        cos_even, sin_even, cos_odd, sin_odd = sums
        cos_sum, cos_gap = plus(cos_even, cos_odd), minus(cos_even, cos_odd)
        sin_sum, sin_gap = plus(sin_even, sin_odd), minus(sin_even, sin_odd)
        out[step] = plus(cos_sum, sin_sum)
        out[(16 + step) % 32] = plus(cos_gap, sin_gap)
        if step:
            out[32 - step] = minus(cos_sum, sin_sum)
            out[16 - step] = minus(cos_gap, sin_gap)
    return out


def gather_lines(points, upper):
    out = [None] * LINES
    for parity in range(2):
        sign = 1 - 2 * parity
        folded = [
            points[step] + points[step + 16] if sign > 0 else points[step] - points[step + 16]
            for step in range(16)
        ]
        even, odd = [folded[0]], [None]
        for step in range(1, 8):
            mirror = folded[16 - step]
            even.append(folded[step] + mirror if sign > 0 else folded[step] - mirror)
            odd.append(
                turned(folded[step] - mirror if sign > 0 else folded[step] + mirror, upper)
            )
        even.append(folded[8])
        odd.append(turned(folded[8], upper))
        for l in range(parity, LINES, 2):
            terms = [scaled(cosine_of(l * step, 32), even[step]) for step in range(9)]
            terms += [scaled(-sine_of(l * step, 32), odd[step]) for step in range(1, 9)]
            out[l] = total(terms)
    return out


def section_kernel(
    start_field,
    section_field,
    start_term,
    first_term,
    second_term,
    first_table,
    second_table,
    third_table,
    last_table,
    line_turns,
    base,
    target,
    sent_one,
    got_one,
    sent_two,
    got_two,
    sent_three,
    got_three,
    sent_four,
    got_four,
    lines_high,
    lines_low,
    lines_full,
    lines_imag,
    points,
    table_high,
    table_low,
    back_high,
    back_low,
    weight_last,
    send_sems,
    recv_sems,
):
    row, col = lax.axis_index("row"), lax.axis_index("col")
    own = col * ROWS + row
    lower_half = row < KEPT // 2
    holds = (col < LINES) & (lower_half | (row >= ROWS - KEPT // 2))
    kept_row = jnp.where(lower_half, row, jnp.where(row >= ROWS - KEPT // 2, row - 4, 0))
    kept_col = jnp.where(col < LINES, col, 0)

    def copy(source, destination, phase, peer_row, peer_col):
        return pltpu.make_async_remote_copy(
            source,
            destination,
            send_sems.at[phase],
            recv_sems.at[phase],
            device_id={"row": peer_row, "col": peer_col},
            device_id_type=pl.DeviceIdType.MESH,
        )

    def await_bytes(ref, sems, phase):
        pltpu.make_async_copy(ref, ref, sems.at[phase]).wait()

    def shuffle(group, carry):
        for part in range(2):
            for quarter in range(4):
                start = pl.multiple_of(group * 64, 64) + (part * 4 + quarter)
                sent_one[pl.ds(start, 8, stride=8), :] = section_field[
                    part,
                    pl.ds(pl.multiple_of(group * 8, 8), 8),
                    quarter * 128 : quarter * 128 + 128,
                ]
        return carry

    @pl.when(holds)
    def _():
        lax.fori_loop(0, BLOCK_X // 8, shuffle, 0)

        def send(step, carry):
            peer_row = lax.rem(row + step % ROWS, ROWS)
            peer_col = lax.rem(col + step // ROWS, COLS)
            copy(
                sent_one.at[pl.ds(pl.multiple_of((peer_col * ROWS + peer_row) * 8, 8), 8)],
                got_one.at[kept_col, pl.ds(pl.multiple_of(kept_row * 8, 8), 8)],
                0,
                peer_row,
                peer_col,
            ).start()
            return carry

        lax.fori_loop(1, DEVICES, send, 0)
        pltpu.make_async_copy(
            sent_one.at[pl.ds(pl.multiple_of(own * 8, 8), 8)],
            got_one.at[kept_col, pl.ds(pl.multiple_of(kept_row * 8, 8), 8)],
            recv_sems.at[0],
        ).start()

    def turn_tables(flip):
        high, low = (back_high, back_low) if flip else (table_high, table_low)

        def step(index, carry):
            cosine, sine = carry
            for place, value in enumerate((cosine, sine)):
                top, rest = split(value)
                if flip:
                    high[index, 128 * place : 128 * place + 128, :] = top
                    low[index, 128 * place : 128 * place + 128, :] = rest
                else:
                    high[index, :, 128 * place : 128 * place + 128] = top
                    low[index, :, 128 * place : 128 * place + 128] = rest
            spin_cos, spin_sin = base[2 + 2 * flip], base[3 + 2 * flip]
            return (
                cosine * spin_cos - sine * spin_sin,
                cosine * spin_sin + sine * spin_cos,
            )

        lax.fori_loop(0, PAIRS, step, (base[0], base[1]))

    turn_tables(0)

    await_bytes(got_one, recv_sems, 0)

    def wave_of(rows_shape):
        rows = lax.broadcasted_iota(jnp.int32, rows_shape, 0)
        lanes = lax.broadcasted_iota(jnp.int32, rows_shape, 1)
        block = lax.shift_right_logical(rows, 3)
        block = jnp.where(block < KEPT // 2, block, block + (ROWS - KEPT))
        index_y = block * BLOCK_Y + lax.bitwise_and(rows, 3) * 128 + lanes
        return jnp.where(index_y < LENGTH // 2, index_y, index_y - LENGTH)

    wave_y = wave_of((KEPT * 8, 128))
    kappa_y = wave_scale * wave_y.astype(FULL) / LENGTH
    keep_y = 3 * jnp.abs(wave_y) < LENGTH
    turn_cos = jnp.concatenate([line_turns[0], line_turns[0]], axis=1)
    turn_sin = jnp.concatenate([line_turns[1], line_turns[1]], axis=1)

    def line_in(l, carry):
        wave_x = l * BLOCK_X + own
        full_x = jnp.full((1, 128), wave_x, jnp.int32)
        kappa_x = wave_scale * full_x.astype(FULL) / LENGTH
        square = full_x * full_x + wave_y * wave_y
        inverse_sq = LENGTH * LENGTH / (9.0 * jnp.maximum(square, 1).astype(FULL))
        doubled = jnp.where(full_x == 0, 1.0, 2.0) * (1.0 / LENGTH)
        keep = keep_y & (3 * full_x < LENGTH)
        factor = jnp.where(keep, inverse_sq * doubled, 0.0)
        data = got_one[l]
        both = jnp.concatenate(
            [kappa_y * factor * data, -(kappa_x * factor) * data], axis=1
        )
        high, low = split(both)
        mixed = times(first_table[0], first_table[1], high, low)
        real, imag = mixed[:64], mixed[64:]
        out_real = real * turn_cos - imag * turn_sin
        out_imag = real * turn_sin + imag * turn_cos
        top, rest = split(jnp.concatenate([out_real, out_imag], axis=1))
        place = pl.ds(pl.multiple_of(l * 64, 64), 64)
        lines_high[place, :] = top
        lines_low[place, :] = rest
        return carry

    lax.fori_loop(0, LINES, line_in, 0)

    for quarter in range(4):
        if quarter % 2 == 0:
            wide = slice(128 * quarter, 128 * quarter + 256)
            lines_full[...] = times(
                lines_high[...],
                lines_low[...],
                second_table[0, :, wide],
                second_table[1, :, wide],
            )
        inner = slice(128 * (quarter % 2), 128 * (quarter % 2) + 128)

        def place_line(l, carry):
            for group in range(8):
                sent_two[
                    pl.ds((quarter * 64 + group * 8) * LINES + l, 8, stride=LINES), :
                ] = lines_full[
                    pl.ds(pl.multiple_of(l * 64, 64) + group * 8, 8), inner
                ]
            return carry

        lax.fori_loop(0, LINES, place_line, 0)

    def exchange(source, destination, phase):
        def send(step, carry):
            peer_row = lax.rem(row + step % ROWS, ROWS)
            peer_col = lax.rem(col + step // ROWS, COLS)
            copy(
                source.at[pl.ds((peer_col * ROWS + peer_row) * LINES, LINES)],
                destination.at[pl.ds(own * LINES, LINES)],
                phase,
                peer_row,
                peer_col,
            ).start()
            return carry

        lax.fori_loop(1, DEVICES, send, 0)
        pltpu.make_async_copy(
            source.at[pl.ds(own * LINES, LINES)],
            destination.at[pl.ds(own * LINES, LINES)],
            recv_sems.at[phase],
        ).start()

    exchange(sent_two, got_two, 1)

    def linear(group, carry):
        place = pl.ds(pl.multiple_of(group * 8, 8), 8)
        shape = (8, BLOCK_Y)
        wave_x = col * BLOCK_X + group * 8 + lax.broadcasted_iota(jnp.int32, shape, 0)
        index_y = row * BLOCK_Y + lax.broadcasted_iota(jnp.int32, shape, 1)
        signed_y = jnp.where(index_y < LENGTH // 2, index_y, index_y - LENGTH)
        damping, weight_a, weight_b, weight_c = section_weights(wave_x, signed_y)
        weight_last[place, :] = weight_c
        for part in range(2):
            target[part, place, :] = (
                damping * start_field[part, place, :]
                + weight_a * start_term[part, place, :]
                + 2.0 * weight_b * (first_term[part, place, :] + second_term[part, place, :])
            )
        return carry

    lax.fori_loop(0, BLOCK_X // 8, linear, 0)
    turn_tables(1)

    await_bytes(got_two, recv_sems, 1)

    lane = lax.broadcasted_iota(jnp.int32, (8, 128), 1)
    upper = lane >= 64

    def columns_in(group, carry):
        spread = []
        for high_bit in range(2):
            start = (high_bit * 128 + group * 8) * LINES
            spread.append(
                spread_lines(
                    [got_two[pl.ds(start + l, 8, stride=LINES), :] for l in range(LINES)],
                    upper,
                )
            )
        column = [None] * 64
        for step in range(32):
            other = spread[1][step]
            moved = total(
                [
                    scaled(cosine_of(step, 64), other),
                    scaled(sine_of(step, 64), turned(other, upper)) if step else None,
                ]
            )
            column[step] = spread[0][step] + moved
            column[step + 32] = spread[0][step] - moved
        place = pl.multiple_of(group * 8, 8)
        for step in range(PAIRS):
            value = column[step]
            if step % 32 == 0:
                real_part = jnp.where(upper, 0.0, value)
                imag_part = jnp.where(upper, 0.0, pltpu.roll(value, 64, 1))
            else:
                mirror = column[64 - step]
                real_part = jnp.where(upper, pltpu.roll(mirror, 64, 1), value)
                imag_part = jnp.where(upper, -mirror, pltpu.roll(value, 64, 1))
            points[step, pl.ds(place, 8), :] = real_part
            points[step, pl.ds(place + 128, 8), :] = imag_part
        return carry

    lax.fori_loop(0, 16, columns_in, 0)

    first_field = lax.broadcasted_iota(jnp.int32, (128, 128), 1) % 64 < 32

    def column_products(index, carry):
        high, low = split(points[index])
        grid = times(table_high[index], table_low[index], high, low)
        from_left = pltpu.roll(grid, 32, 1)
        from_right = pltpu.roll(grid, 96, 1)
        product = jnp.where(
            first_field, grid * from_right, (grid - from_left) * (grid + from_left)
        )
        high, low = split(product)
        points[index] = times(back_high[index], back_low[index], high, low)
        return carry

    lax.fori_loop(0, PAIRS, column_products, 0)

    def columns_out(group, carry):
        place = pl.multiple_of(group * 8, 8)
        column = [None] * 64
        for step in range(PAIRS):
            real_part = points[step, pl.ds(place, 8), :]
            imag_part = points[step, pl.ds(place + 128, 8), :]
            column[step] = jnp.where(upper, pltpu.roll(imag_part, 64, 1), real_part)
            if step % 32:
                column[64 - step] = jnp.where(
                    upper, -imag_part, pltpu.roll(real_part, 64, 1)
                )
        sums, gaps = [], []
        for step in range(32):
            sums.append(column[step] + column[step + 32])
            gap = column[step] - column[step + 32]
            gaps.append(
                total(
                    [
                        scaled(cosine_of(step, 64), gap),
                        scaled(-sine_of(step, 64), turned(gap, upper)) if step else None,
                    ]
                )
            )
        for high_bit, values in enumerate((sums, gaps)):
            start = (high_bit * 128 + group * 8) * LINES
            for l, value in enumerate(gather_lines(values, upper)):
                sent_three[pl.ds(start + l, 8, stride=LINES), :] = value
        return carry

    lax.fori_loop(0, 16, columns_out, 0)

    exchange(sent_three, got_three, 2)
    await_bytes(got_three, recv_sems, 2)

    def collect(l, carry):
        for quarter in range(4):
            for group in range(4):
                start = (quarter * 64 + group * 16) * LINES + l
                top, rest = split(
                    jnp.concatenate(
                        [
                            got_three[pl.ds(start, 8, stride=LINES), :],
                            got_three[pl.ds(start + 8 * LINES, 8, stride=LINES), :],
                        ]
                    )
                )
                place = pl.ds(pl.multiple_of(l * 64, 64) + group * 16, 16)
                lanes = slice(quarter * 128, quarter * 128 + 128)
                lines_high[place, lanes] = top
                lines_low[place, lanes] = rest
        return carry

    lax.fori_loop(0, LINES, collect, 0)

    for part, full in enumerate((lines_full, lines_imag)):
        wide = slice(256 * part, 256 * part + 256)
        full[...] = times(
            lines_high[...], lines_low[...], third_table[0, :, wide], third_table[1, :, wide]
        )

    def line_out(l, carry):
        place = pl.ds(pl.multiple_of(l * 64, 64), 64)
        real, imag = lines_full[place, :], lines_imag[place, :]
        out_real = real * turn_cos + imag * turn_sin
        out_imag = imag * turn_cos - real * turn_sin
        high, low = split(jnp.concatenate([out_real, out_imag], axis=0))
        value = times(last_table[0], last_table[1], high, low)
        full_x = jnp.full((1, 128), l * BLOCK_X + own, jnp.int32)
        kappa_x = wave_scale * full_x.astype(FULL) / LENGTH
        scale = jnp.where(keep_y & (3 * full_x < LENGTH), 1.0 / LENGTH, 0.0)
        weight_cross = (kappa_x * kappa_x - kappa_y * kappa_y) * scale
        weight_gap = kappa_x * kappa_y * scale
        sent_four[l] = weight_cross * value[:, :128] + weight_gap * value[:, 128:]
        return carry

    lax.fori_loop(0, LINES, line_out, 0)

    def send_term(step, carry):
        peer_col = lax.rem(kept_col + step // KEPT, LINES)
        block = lax.rem(kept_row + step % KEPT, KEPT)
        peer_row = jnp.where(block < KEPT // 2, block, block + (ROWS - KEPT))
        block_rows = pl.ds(pl.multiple_of(block * 8, 8), 8)
        target_rows = pl.ds(pl.multiple_of(own * 8, 8), 8)
        itself = (peer_row == row) & (peer_col == col)

        @pl.when(itself)
        def _():
            pltpu.make_async_copy(
                sent_four.at[peer_col, block_rows], got_four.at[target_rows], recv_sems.at[3]
            ).start()

        @pl.when(jnp.logical_not(itself))
        def _():
            copy(
                sent_four.at[peer_col, block_rows],
                got_four.at[target_rows],
                3,
                peer_row,
                peer_col,
            ).start()

        return carry

    lax.fori_loop(0, LINES * KEPT, send_term, 0)

    @pl.when(holds)
    def _():
        await_bytes(got_four, recv_sems, 3)

        def finish(group, carry):
            place = pl.ds(pl.multiple_of(group * 8, 8), 8)
            for part in range(2):
                for quarter in range(4):
                    lanes = slice(quarter * 128, quarter * 128 + 128)
                    start = pl.multiple_of(group * 64, 64) + (part * 4 + quarter)
                    target[part, place, lanes] = (
                        target[part, place, lanes]
                        + weight_last[place, lanes] * got_four[pl.ds(start, 8, stride=8), :]
                    )
            return carry

        lax.fori_loop(0, BLOCK_X // 8, finish, 0)
        others = sent_one.at[pl.ds(0, (DEVICES - 1) * 8)]
        await_bytes(others, send_sems, 0)
        await_bytes(sent_four.at[0, pl.ds(0, KEPT * 8 - 8)], send_sems, 3)
        await_bytes(sent_four.at[pl.ds(0, LINES - 1)], send_sems, 3)

    @pl.when(jnp.logical_not(holds))
    def _():
        await_bytes(sent_four, send_sems, 3)

    for phase, sent in ((1, sent_two), (2, sent_three)):
        await_bytes(sent.at[pl.ds(0, (DEVICES - 1) * LINES)], send_sems, phase)


def per_device(start_field, section_field, start_term, first_term, second_term):
    shape = (2, BLOCK_X, BLOCK_Y)
    fields = [
        field.reshape(shape)
        for field in (start_field, section_field, start_term, first_term, second_term)
    ]
    constants = [jnp.asarray(table) for table in tables()]
    vmem = pl.BlockSpec(memory_space=pltpu.VMEM)
    result = pl.pallas_call(
        section_kernel,
        out_shape=jax.ShapeDtypeStruct(shape, FULL),
        in_specs=[vmem] * (len(fields) + len(constants)),
        out_specs=vmem,
        scratch_shapes=[
            pltpu.VMEM((BLOCK_X * 8, 128), FULL),
            pltpu.VMEM((LINES, KEPT * 8, 128), FULL),
            pltpu.VMEM((DEVICES * LINES, 128), FULL),
            pltpu.VMEM((DEVICES * LINES, 128), FULL),
            pltpu.VMEM((DEVICES * LINES, 128), FULL),
            pltpu.VMEM((DEVICES * LINES, 128), FULL),
            pltpu.VMEM((LINES, KEPT * 8, 128), FULL),
            pltpu.VMEM((BLOCK_X * 8, 128), FULL),
            pltpu.VMEM((LINES * 64, 512), HIGH),
            pltpu.VMEM((LINES * 64, 512), HIGH),
            pltpu.VMEM((LINES * 64, 256), FULL),
            pltpu.VMEM((LINES * 64, 256), FULL),
            pltpu.VMEM((PAIRS, 256, 128), FULL),
            pltpu.VMEM((PAIRS, 128, 256), HIGH),
            pltpu.VMEM((PAIRS, 128, 256), HIGH),
            pltpu.VMEM((PAIRS, 256, 128), HIGH),
            pltpu.VMEM((PAIRS, 256, 128), HIGH),
            pltpu.VMEM((BLOCK_X, BLOCK_Y), FULL),
            pltpu.SemaphoreType.DMA((4,)),
            pltpu.SemaphoreType.DMA((4,)),
        ],
        compiler_params=pltpu.CompilerParams(
            has_side_effects=True, vmem_limit_bytes=56 * 2**20
        ),
        name="section",
    )(*fields, *constants)
    return result.reshape((1,) + shape)


def solution(mesh):
    spec = P(None, None, "col", "row")
    return jax.shard_map(
        per_device,
        mesh=mesh,
        in_specs=(spec,) * 5,
        out_specs=spec,
        check_vma=False,
    )
```

profile of v0, /device:TPU:1, one launch (start us, length us, event | category | flops | bytes accessed | tf_op | source)
XLA Modules:
  0.0 175.8 jit_solution(6974487675418763113)
XLA Ops:
  0.0 173.5 %section.1 = f32[2,256,512]{2,1,0:T(8,128)} custom-call(f32[2,256,512]{2,1,0:T(8,128)} %bitcast.7, f32[2,256,512]{2,1,0:T(8,128)} %bitcast.8, f32[2,256,512]{2,1,0:T(8,128)} %bitcast.9, f32[2,256,512]{2,1,0:T(8,128)} %bitcast.10, f32[2,256,512]{2,1,0:T(8,128)} %bitcast.11, bf16[2,128,96]{2,1,0:T(8,128)(2,1)} %constant.12.clone.first_table, ...), custom_call_target="tpu_custom_call" | custom-call | tf_op jit(solution)/shard_map/section/pallas_call | solution.py:615
  173.5 2.3 %copy.13 = f32[1,2,256,512]{3,2,1,0:T(8,128)} copy(f32[1,2,256,512]{3,2,1,0:T(8,128)} %bitcast.6) | data formatting | bytes 2097152
where the time goes:
time: 176 us
  Pallas kernels  174 us (99%)
  local copies, waits for them, and re-layouts  2.26 us (1%)
    pallas_call x1, Pallas kernels, per_device(): pl.pallas_call(section_kernel, out_shape=jax.ShapeDtypeStruct(shape, FULL...  174 us

commit v1 on v0

--- a/solution.py
+++ b/solution.py
@@ -98,7 +98,10 @@
     base = np.stack(
         [cosine, -sine, np.cos(spin), -np.sin(spin), np.cos(spin.T), -np.sin(spin.T)]
     ).astype(np.float32)
-    return halves(first), halves(second), halves(second.T), halves(last), turns, base
+    wide = np.stack(
+        [np.concatenate(halves(second[:, 128 * g : 128 * g + 128]), axis=1) for g in range(4)]
+    )
+    return halves(first), wide, halves(second.T), halves(last), turns, base
 
 
 def split(values):
@@ -221,33 +224,42 @@
     lines_full,
     lines_imag,
     points,
-    table_high,
-    table_low,
-    back_high,
-    back_low,
+    table,
+    back,
     weight_last,
     send_sems,
     recv_sems,
+    line_sems,
+    column_sems,
 ):
     row, col = lax.axis_index("row"), lax.axis_index("col")
     own = col * ROWS + row
+    own_line = col * 8 + lax.rem(row, 8) + 128 * (row // 8)
     lower_half = row < KEPT // 2
     holds = (col < LINES) & (lower_half | (row >= ROWS - KEPT // 2))
     kept_row = jnp.where(lower_half, row, jnp.where(row >= ROWS - KEPT // 2, row - 4, 0))
     kept_col = jnp.where(col < LINES, col, 0)
 
-    def copy(source, destination, phase, peer_row, peer_col):
-        return pltpu.make_async_remote_copy(
-            source,
-            destination,
-            send_sems.at[phase],
-            recv_sems.at[phase],
-            device_id={"row": peer_row, "col": peer_col},
-            device_id_type=pl.DeviceIdType.MESH,
-        )
-
-    def await_bytes(ref, sems, phase):
-        pltpu.make_async_copy(ref, ref, sems.at[phase]).wait()
+    def post(source, destination, phase, peer_row, peer_col, sem):
+        itself = (peer_row == row) & (peer_col == col)
+
+        @pl.when(itself)
+        def _():
+            pltpu.make_async_copy(source, destination, sem).start()
+
+        @pl.when(jnp.logical_not(itself))
+        def _():
+            pltpu.make_async_remote_copy(
+                source,
+                destination,
+                send_sems.at[phase],
+                sem,
+                device_id={"row": peer_row, "col": peer_col},
+                device_id_type=pl.DeviceIdType.MESH,
+            ).start()
+
+    def await_bytes(ref, sem):
+        pltpu.make_async_copy(ref, ref, sem).wait()
 
     def shuffle(group, carry):
         for part in range(2):
@@ -267,35 +279,31 @@
         def send(step, carry):
             peer_row = lax.rem(row + step % ROWS, ROWS)
             peer_col = lax.rem(col + step // ROWS, COLS)
-            copy(
-                sent_one.at[pl.ds(pl.multiple_of((peer_col * ROWS + peer_row) * 8, 8), 8)],
+            line = peer_col * 8 + lax.rem(peer_row, 8) + 128 * (peer_row // 8)
+            post(
+                sent_one.at[pl.ds(pl.multiple_of(line * 8, 8), 8)],
                 got_one.at[kept_col, pl.ds(pl.multiple_of(kept_row * 8, 8), 8)],
                 0,
                 peer_row,
                 peer_col,
-            ).start()
+                line_sems.at[kept_col],
+            )
             return carry
 
-        lax.fori_loop(1, DEVICES, send, 0)
-        pltpu.make_async_copy(
-            sent_one.at[pl.ds(pl.multiple_of(own * 8, 8), 8)],
-            got_one.at[kept_col, pl.ds(pl.multiple_of(kept_row * 8, 8), 8)],
-            recv_sems.at[0],
-        ).start()
+        lax.fori_loop(0, DEVICES, send, 0)
 
     def turn_tables(flip):
-        high, low = (back_high, back_low) if flip else (table_high, table_low)
-
         def step(index, carry):
             cosine, sine = carry
             for place, value in enumerate((cosine, sine)):
                 top, rest = split(value)
+                span = slice(128 * place, 128 * place + 128)
                 if flip:
-                    high[index, 128 * place : 128 * place + 128, :] = top
-                    low[index, 128 * place : 128 * place + 128, :] = rest
+                    back[index, span, 0:128] = top
+                    back[index, span, 128:256] = rest
                 else:
-                    high[index, :, 128 * place : 128 * place + 128] = top
-                    low[index, :, 128 * place : 128 * place + 128] = rest
+                    table[index, 0:128, span] = top
+                    table[index, 128:256, span] = rest
             spin_cos, spin_sin = base[2 + 2 * flip], base[3 + 2 * flip]
             return (
                 cosine * spin_cos - sine * spin_sin,
@@ -305,8 +313,6 @@
         lax.fori_loop(0, PAIRS, step, (base[0], base[1]))
 
     turn_tables(0)
-
-    await_bytes(got_one, recv_sems, 0)
 
     def wave_of(rows_shape):
         rows = lax.broadcasted_iota(jnp.int32, rows_shape, 0)
@@ -322,8 +328,9 @@
     turn_cos = jnp.concatenate([line_turns[0], line_turns[0]], axis=1)
     turn_sin = jnp.concatenate([line_turns[1], line_turns[1]], axis=1)
 
-    def line_in(l, carry):
-        wave_x = l * BLOCK_X + own
+    def line_in(l):
+        await_bytes(got_one.at[l], line_sems.at[l])
+        wave_x = l * BLOCK_X + own_line
         full_x = jnp.full((1, 128), wave_x, jnp.int32)
         kappa_x = wave_scale * full_x.astype(FULL) / LENGTH
         square = full_x * full_x + wave_y * wave_y
@@ -344,53 +351,59 @@
         place = pl.ds(pl.multiple_of(l * 64, 64), 64)
         lines_high[place, :] = top
         lines_low[place, :] = rest
-        return carry
-
-    lax.fori_loop(0, LINES, line_in, 0)
-
-    for quarter in range(4):
-        if quarter % 2 == 0:
-            wide = slice(128 * quarter, 128 * quarter + 256)
-            lines_full[...] = times(
-                lines_high[...],
-                lines_low[...],
-                second_table[0, :, wide],
-                second_table[1, :, wide],
-            )
-        inner = slice(128 * (quarter % 2), 128 * (quarter % 2) + 128)
-
-        def place_line(l, carry):
-            for group in range(8):
-                sent_two[
-                    pl.ds((quarter * 64 + group * 8) * LINES + l, 8, stride=LINES), :
-                ] = lines_full[
-                    pl.ds(pl.multiple_of(l * 64, 64) + group * 8, 8), inner
-                ]
-            return carry
-
-        lax.fori_loop(0, LINES, place_line, 0)
-
-    def exchange(source, destination, phase):
+
+    def line_step(step, carry):
+        l = lax.rem(col + COLS - step, COLS)
+
+        @pl.when(l < LINES)
+        def _():
+            line_in(l)
+
+        return carry
+
+    lax.fori_loop(0, COLS, line_step, 0)
+
+    def post_column(source, destination, phase, peer_col, sem):
         def send(step, carry):
-            peer_row = lax.rem(row + step % ROWS, ROWS)
-            peer_col = lax.rem(col + step // ROWS, COLS)
-            copy(
+            peer_row = lax.rem(row + step, ROWS)
+            post(
                 source.at[pl.ds((peer_col * ROWS + peer_row) * LINES, LINES)],
                 destination.at[pl.ds(own * LINES, LINES)],
                 phase,
                 peer_row,
                 peer_col,
-            ).start()
+                sem,
+            )
             return carry
 
-        lax.fori_loop(1, DEVICES, send, 0)
-        pltpu.make_async_copy(
-            source.at[pl.ds(own * LINES, LINES)],
-            destination.at[pl.ds(own * LINES, LINES)],
-            recv_sems.at[phase],
-        ).start()
-
-    exchange(sent_two, got_two, 1)
+        lax.fori_loop(0, ROWS, send, 0)
+
+    def quarter_out(step, carry):
+        quarter = lax.rem(col // 4 + step, 4)
+        high_part = jnp.dot(lines_high[...], second_table[quarter], preferred_element_type=FULL)
+        low_part = jnp.dot(
+            lines_low[...], second_table[quarter, :, 0:128], preferred_element_type=FULL
+        )
+        lines_full[:, 0:128] = (high_part[:, 128:256] + low_part) + high_part[:, 0:128]
+
+        def place_line(l, inner):
+            for group in range(8):
+                sent_two[
+                    pl.ds((quarter * 64 + group * 8) * LINES + l, 8, stride=LINES), :
+                ] = lines_full[pl.ds(pl.multiple_of(l * 64, 64) + group * 8, 8), 0:128]
+            return inner
+
+        lax.fori_loop(0, LINES, place_line, 0)
+
+        def send_quarter(offset, inner):
+            peer_col = quarter * 4 + lax.rem(col + offset, 4)
+            post_column(sent_two, got_two, 1, peer_col, column_sems.at[col])
+            return inner
+
+        lax.fori_loop(0, 4, send_quarter, 0)
+        return carry
+
+    lax.fori_loop(0, 4, quarter_out, 0)
 
     def linear(group, carry):
         place = pl.ds(pl.multiple_of(group * 8, 8), 8)
@@ -411,15 +424,19 @@
     lax.fori_loop(0, BLOCK_X // 8, linear, 0)
     turn_tables(1)
 
-    await_bytes(got_two, recv_sems, 1)
-
     lane = lax.broadcasted_iota(jnp.int32, (8, 128), 1)
     upper = lane >= 64
 
-    def columns_in(group, carry):
+    def columns_in(step_in, carry):
+        group = 4 * lax.rem(col // 4 + 4 - step_in // 4, 4) + lax.rem(
+            col + 4 - step_in % 4, 4
+        )
+        await_bytes(
+            got_two.at[pl.ds(group * ROWS * LINES, ROWS * LINES)], column_sems.at[group]
+        )
         spread = []
         for high_bit in range(2):
-            start = (high_bit * 128 + group * 8) * LINES
+            start = (high_bit * 8 + group * 16) * LINES
             spread.append(
                 spread_lines(
                     [got_two[pl.ds(start + l, 8, stride=LINES), :] for l in range(LINES)],
@@ -455,21 +472,33 @@
 
     first_field = lax.broadcasted_iota(jnp.int32, (128, 128), 1) % 64 < 32
 
-    def column_products(index, carry):
-        high, low = split(points[index])
-        grid = times(table_high[index], table_low[index], high, low)
-        from_left = pltpu.roll(grid, 32, 1)
-        from_right = pltpu.roll(grid, 96, 1)
-        product = jnp.where(
-            first_field, grid * from_right, (grid - from_left) * (grid + from_left)
-        )
-        high, low = split(product)
-        points[index] = times(back_high[index], back_low[index], high, low)
-        return carry
-
-    lax.fori_loop(0, PAIRS, column_products, 0)
-
-    def columns_out(group, carry):
+    def column_products(step, carry):
+        for index in (3 * step, 3 * step + 1, 3 * step + 2):
+            high, low = split(points[index])
+            wide = jnp.dot(
+                table[index],
+                jnp.concatenate([high, low], axis=1),
+                preferred_element_type=FULL,
+            )
+            grid = (wide[:128, 128:] + wide[128:, :128]) + wide[:128, :128]
+            from_left = pltpu.roll(grid, 32, 1)
+            from_right = pltpu.roll(grid, 96, 1)
+            product = jnp.where(
+                first_field, grid * from_right, (grid - from_left) * (grid + from_left)
+            )
+            both = jnp.concatenate(split(product), axis=1)
+            wide = jnp.dot(
+                back[index],
+                jnp.concatenate([both, both], axis=0),
+                preferred_element_type=FULL,
+            )
+            points[index] = wide[:, 128:] + wide[:, :128]
+        return carry
+
+    lax.fori_loop(0, PAIRS // 3, column_products, 0)
+
+    def columns_out(step_out, carry):
+        group = lax.rem(col + step_out, COLS)
         place = pl.multiple_of(group * 8, 8)
         column = [None] * 64
         for step in range(PAIRS):
@@ -493,15 +522,15 @@
                 )
             )
         for high_bit, values in enumerate((sums, gaps)):
-            start = (high_bit * 128 + group * 8) * LINES
+            start = (high_bit * 8 + group * 16) * LINES
             for l, value in enumerate(gather_lines(values, upper)):
                 sent_three[pl.ds(start + l, 8, stride=LINES), :] = value
+        post_column(sent_three, got_three, 2, group, recv_sems.at[0])
         return carry
 
     lax.fori_loop(0, 16, columns_out, 0)
 
-    exchange(sent_three, got_three, 2)
-    await_bytes(got_three, recv_sems, 2)
+    await_bytes(got_three, recv_sems.at[0])
 
     def collect(l, carry):
         for quarter in range(4):
@@ -529,54 +558,41 @@
             lines_high[...], lines_low[...], third_table[0, :, wide], third_table[1, :, wide]
         )
 
-    def line_out(l, carry):
+    def line_out(step_out, carry):
+        l = lax.rem(kept_col + step_out, LINES)
         place = pl.ds(pl.multiple_of(l * 64, 64), 64)
         real, imag = lines_full[place, :], lines_imag[place, :]
         out_real = real * turn_cos + imag * turn_sin
         out_imag = imag * turn_cos - real * turn_sin
         high, low = split(jnp.concatenate([out_real, out_imag], axis=0))
         value = times(last_table[0], last_table[1], high, low)
-        full_x = jnp.full((1, 128), l * BLOCK_X + own, jnp.int32)
+        full_x = jnp.full((1, 128), l * BLOCK_X + own_line, jnp.int32)
         kappa_x = wave_scale * full_x.astype(FULL) / LENGTH
         scale = jnp.where(keep_y & (3 * full_x < LENGTH), 1.0 / LENGTH, 0.0)
         weight_cross = (kappa_x * kappa_x - kappa_y * kappa_y) * scale
         weight_gap = kappa_x * kappa_y * scale
         sent_four[l] = weight_cross * value[:, :128] + weight_gap * value[:, 128:]
+
+        def send_term(step, inner):
+            block = lax.rem(kept_row + step, KEPT)
+            post(
+                sent_four.at[l, pl.ds(pl.multiple_of(block * 8, 8), 8)],
+                got_four.at[pl.ds(pl.multiple_of(own_line * 8, 8), 8)],
+                3,
+                jnp.where(block < KEPT // 2, block, block + (ROWS - KEPT)),
+                l,
+                recv_sems.at[1],
+            )
+            return inner
+
+        lax.fori_loop(0, KEPT, send_term, 0)
         return carry
 
     lax.fori_loop(0, LINES, line_out, 0)
-
-    def send_term(step, carry):
-        peer_col = lax.rem(kept_col + step // KEPT, LINES)
-        block = lax.rem(kept_row + step % KEPT, KEPT)
-        peer_row = jnp.where(block < KEPT // 2, block, block + (ROWS - KEPT))
-        block_rows = pl.ds(pl.multiple_of(block * 8, 8), 8)
-        target_rows = pl.ds(pl.multiple_of(own * 8, 8), 8)
-        itself = (peer_row == row) & (peer_col == col)
-
-        @pl.when(itself)
-        def _():
-            pltpu.make_async_copy(
-                sent_four.at[peer_col, block_rows], got_four.at[target_rows], recv_sems.at[3]
-            ).start()
-
-        @pl.when(jnp.logical_not(itself))
-        def _():
-            copy(
-                sent_four.at[peer_col, block_rows],
-                got_four.at[target_rows],
-                3,
-                peer_row,
-                peer_col,
-            ).start()
-
-        return carry
-
-    lax.fori_loop(0, LINES * KEPT, send_term, 0)
 
     @pl.when(holds)
     def _():
-        await_bytes(got_four, recv_sems, 3)
+        await_bytes(got_four, recv_sems.at[1])
 
         def finish(group, carry):
             place = pl.ds(pl.multiple_of(group * 8, 8), 8)
@@ -592,16 +608,16 @@
 
         lax.fori_loop(0, BLOCK_X // 8, finish, 0)
         others = sent_one.at[pl.ds(0, (DEVICES - 1) * 8)]
-        await_bytes(others, send_sems, 0)
-        await_bytes(sent_four.at[0, pl.ds(0, KEPT * 8 - 8)], send_sems, 3)
-        await_bytes(sent_four.at[pl.ds(0, LINES - 1)], send_sems, 3)
+        await_bytes(others, send_sems.at[0])
+        await_bytes(sent_four.at[0, pl.ds(0, KEPT * 8 - 8)], send_sems.at[3])
+        await_bytes(sent_four.at[pl.ds(0, LINES - 1)], send_sems.at[3])
 
     @pl.when(jnp.logical_not(holds))
     def _():
-        await_bytes(sent_four, send_sems, 3)
+        await_bytes(sent_four, send_sems.at[3])
 
     for phase, sent in ((1, sent_two), (2, sent_three)):
-        await_bytes(sent.at[pl.ds(0, (DEVICES - 1) * LINES)], send_sems, phase)
+        await_bytes(sent.at[pl.ds(0, (DEVICES - 1) * LINES)], send_sems.at[phase])
 
 
 def per_device(start_field, section_field, start_term, first_term, second_term):
@@ -631,13 +647,13 @@
             pltpu.VMEM((LINES * 64, 256), FULL),
             pltpu.VMEM((LINES * 64, 256), FULL),
             pltpu.VMEM((PAIRS, 256, 128), FULL),
-            pltpu.VMEM((PAIRS, 128, 256), HIGH),
-            pltpu.VMEM((PAIRS, 128, 256), HIGH),
-            pltpu.VMEM((PAIRS, 256, 128), HIGH),
-            pltpu.VMEM((PAIRS, 256, 128), HIGH),
+            pltpu.VMEM((PAIRS, 256, 256), HIGH),
+            pltpu.VMEM((PAIRS, 256, 256), HIGH),
             pltpu.VMEM((BLOCK_X, BLOCK_Y), FULL),
             pltpu.SemaphoreType.DMA((4,)),
-            pltpu.SemaphoreType.DMA((4,)),
+            pltpu.SemaphoreType.DMA((2,)),
+            pltpu.SemaphoreType.DMA((LINES,)),
+            pltpu.SemaphoreType.DMA((COLS,)),
         ],
         compiler_params=pltpu.CompilerParams(
             has_side_effects=True, vmem_limit_bytes=56 * 2**20

time: 176 us -> 151 us (0.86)
  Pallas kernels: 174 us -> 149 us
    pallas_call x1, Pallas kernels: 174 us -> 149 us  [per_device(): pl.pallas_call(section_kernel, out_shape=jax.ShapeDtypeStruct(shape, FULL...]
where the time goes in v1:
time: 151 us
  Pallas kernels  149 us (99%)
  local copies, waits for them, and re-layouts  2.26 us (1%)
    pallas_call x1, Pallas kernels, per_device(): pl.pallas_call(section_kernel, out_shape=jax.ShapeDtypeStruct(shape, FULL...  149 us

profile of v1, /device:TPU:1, one launch (start us, length us, event | category | flops | bytes accessed | tf_op | source)
XLA Modules:
  0.0 150.9 jit_solution(196473875222954199)
XLA Ops:
  0.0 148.6 %section.1 = f32[2,256,512]{2,1,0:T(8,128)} custom-call(f32[2,256,512]{2,1,0:T(8,128)} %bitcast.7, f32[2,256,512]{2,1,0:T(8,128)} %bitcast.8, f32[2,256,512]{2,1,0:T(8,128)} %bitcast.9, f32[2,256,512]{2,1,0:T(8,128)} %bitcast.10, f32[2,256,512]{2,1,0:T(8,128)} %bitcast.11, bf16[2,128,96]{2,1,0:T(8,128)(2,1)} %constant.12.clone.first_table, ...), custom_call_target="tpu_custom_call" | custom-call | tf_op jit(solution)/shard_map/section/pallas_call | solution.py:631
  148.6 2.3 %copy.13 = f32[1,2,256,512]{3,2,1,0:T(8,128)} copy(f32[1,2,256,512]{3,2,1,0:T(8,128)} %bitcast.6) | data formatting | bytes 2097152

commit v2 on v1

--- a/solution.py
+++ b/solution.py
@@ -240,6 +240,19 @@
     kept_row = jnp.where(lower_half, row, jnp.where(row >= ROWS - KEPT // 2, row - 4, 0))
     kept_col = jnp.where(col < LINES, col, 0)
 
+    def far_first(step):
+        back_step = 3 - step
+        return lax.bitwise_xor(back_step, lax.shift_right_logical(back_step, 1))
+
+    def col_at(step, sign):
+        across = lax.rem(col // 4 + 4 + sign * far_first(step // 4), 4)
+        along = lax.rem(lax.rem(col, 4) + 4 + sign * far_first(lax.rem(step, 4)), 4)
+        return 4 * across + along
+
+    def row_at(step):
+        across = lax.rem(row // 4 + far_first(step // 4), 4)
+        return 4 * across + lax.bitwise_xor(lax.rem(row, 4), 3 - lax.rem(step, 4))
+
     def post(source, destination, phase, peer_row, peer_col, sem):
         itself = (peer_row == row) & (peer_col == col)
 
@@ -277,8 +290,8 @@
         lax.fori_loop(0, BLOCK_X // 8, shuffle, 0)
 
         def send(step, carry):
-            peer_row = lax.rem(row + step % ROWS, ROWS)
-            peer_col = lax.rem(col + step // ROWS, COLS)
+            peer_row = row_at(lax.rem(step, ROWS))
+            peer_col = col_at(step // ROWS, 1)
             line = peer_col * 8 + lax.rem(peer_row, 8) + 128 * (peer_row // 8)
             post(
                 sent_one.at[pl.ds(pl.multiple_of(line * 8, 8), 8)],
@@ -353,7 +366,7 @@
         lines_low[place, :] = rest
 
     def line_step(step, carry):
-        l = lax.rem(col + COLS - step, COLS)
+        l = col_at(step, -1)
 
         @pl.when(l < LINES)
         def _():
@@ -365,7 +378,7 @@
 
     def post_column(source, destination, phase, peer_col, sem):
         def send(step, carry):
-            peer_row = lax.rem(row + step, ROWS)
+            peer_row = row_at(step)
             post(
                 source.at[pl.ds((peer_col * ROWS + peer_row) * LINES, LINES)],
                 destination.at[pl.ds(own * LINES, LINES)],
@@ -379,7 +392,7 @@
         lax.fori_loop(0, ROWS, send, 0)
 
     def quarter_out(step, carry):
-        quarter = lax.rem(col // 4 + step, 4)
+        quarter = lax.rem(col // 4 + far_first(step), 4)
         high_part = jnp.dot(lines_high[...], second_table[quarter], preferred_element_type=FULL)
         low_part = jnp.dot(
             lines_low[...], second_table[quarter, :, 0:128], preferred_element_type=FULL
@@ -396,7 +409,7 @@
         lax.fori_loop(0, LINES, place_line, 0)
 
         def send_quarter(offset, inner):
-            peer_col = quarter * 4 + lax.rem(col + offset, 4)
+            peer_col = quarter * 4 + lax.rem(col + far_first(offset), 4)
             post_column(sent_two, got_two, 1, peer_col, column_sems.at[col])
             return inner
 
@@ -428,9 +441,7 @@
     upper = lane >= 64
 
     def columns_in(step_in, carry):
-        group = 4 * lax.rem(col // 4 + 4 - step_in // 4, 4) + lax.rem(
-            col + 4 - step_in % 4, 4
-        )
+        group = col_at(step_in, -1)
         await_bytes(
             got_two.at[pl.ds(group * ROWS * LINES, ROWS * LINES)], column_sems.at[group]
         )
@@ -473,7 +484,7 @@
     first_field = lax.broadcasted_iota(jnp.int32, (128, 128), 1) % 64 < 32
 
     def column_products(step, carry):
-        for index in (3 * step, 3 * step + 1, 3 * step + 2):
+        for index in [11 * step + k for k in range(11)]:
             high, low = split(points[index])
             wide = jnp.dot(
                 table[index],
@@ -495,10 +506,10 @@
             points[index] = wide[:, 128:] + wide[:, :128]
         return carry
 
-    lax.fori_loop(0, PAIRS // 3, column_products, 0)
+    lax.fori_loop(0, PAIRS // 11, column_products, 0)
 
     def columns_out(step_out, carry):
-        group = lax.rem(col + step_out, COLS)
+        group = col_at(step_out, 1)
         place = pl.multiple_of(group * 8, 8)
         column = [None] * 64
         for step in range(PAIRS):
@@ -558,8 +569,7 @@
             lines_high[...], lines_low[...], third_table[0, :, wide], third_table[1, :, wide]
         )
 
-    def line_out(step_out, carry):
-        l = lax.rem(kept_col + step_out, LINES)
+    def line_out(l):
         place = pl.ds(pl.multiple_of(l * 64, 64), 64)
         real, imag = lines_full[place, :], lines_imag[place, :]
         out_real = real * turn_cos + imag * turn_sin
@@ -586,9 +596,17 @@
             return inner
 
         lax.fori_loop(0, KEPT, send_term, 0)
-        return carry
-
-    lax.fori_loop(0, LINES, line_out, 0)
+
+    def line_out_step(step, carry):
+        l = col_at(step, 1)
+
+        @pl.when(l < LINES)
+        def _():
+            line_out(l)
+
+        return carry
+
+    lax.fori_loop(0, COLS, line_out_step, 0)
 
     @pl.when(holds)
     def _():

time: 151 us -> 144 us (0.954)
  Pallas kernels: 149 us -> 142 us
    pallas_call x1, Pallas kernels: 149 us -> 142 us  [per_device(): pl.pallas_call(section_kernel, out_shape=jax.ShapeDtypeStruct(shape, FULL...]
where the time goes in v2:
time: 144 us
  Pallas kernels  142 us (99%)
  local copies, waits for them, and re-layouts  2.26 us (2%)
    pallas_call x1, Pallas kernels, per_device(): pl.pallas_call(section_kernel, out_shape=jax.ShapeDtypeStruct(shape, FULL...  142 us

profile of v2, /device:TPU:1, one launch (start us, length us, event | category | flops | bytes accessed | tf_op | source)
XLA Modules:
  0.0 143.8 jit_solution(7613469639847599123)
XLA Ops:
  0.0 141.5 %section.1 = f32[2,256,512]{2,1,0:T(8,128)} custom-call(f32[2,256,512]{2,1,0:T(8,128)} %bitcast.7, f32[2,256,512]{2,1,0:T(8,128)} %bitcast.8, f32[2,256,512]{2,1,0:T(8,128)} %bitcast.9, f32[2,256,512]{2,1,0:T(8,128)} %bitcast.10, f32[2,256,512]{2,1,0:T(8,128)} %bitcast.11, bf16[2,128,96]{2,1,0:T(8,128)(2,1)} %constant.12.clone.first_table, ...), custom_call_target="tpu_custom_call" | custom-call | tf_op jit(solution)/shard_map/section/pallas_call | solution.py:649
  141.5 2.3 %copy.13 = f32[1,2,256,512]{3,2,1,0:T(8,128)} copy(f32[1,2,256,512]{3,2,1,0:T(8,128)} %bitcast.6) | data formatting | bytes 2097152

commit v3 on v2

--- a/solution.py
+++ b/solution.py
@@ -249,6 +249,11 @@
         along = lax.rem(lax.rem(col, 4) + 4 + sign * far_first(lax.rem(step, 4)), 4)
         return 4 * across + along
 
+    def col_far(step, sign):
+        across = lax.rem(col // 4 + 4 + sign * far_first(lax.rem(step, 4)), 4)
+        along = lax.rem(lax.rem(col, 4) + 4 + sign * far_first(step // 4), 4)
+        return 4 * across + along
+
     def row_at(step):
         across = lax.rem(row // 4 + far_first(step // 4), 4)
         return 4 * across + lax.bitwise_xor(lax.rem(row, 4), 3 - lax.rem(step, 4))
@@ -291,7 +296,7 @@
 
         def send(step, carry):
             peer_row = row_at(lax.rem(step, ROWS))
-            peer_col = col_at(step // ROWS, 1)
+            peer_col = col_far(step // ROWS, 1)
             line = peer_col * 8 + lax.rem(peer_row, 8) + 128 * (peer_row // 8)
             post(
                 sent_one.at[pl.ds(pl.multiple_of(line * 8, 8), 8)],
@@ -366,7 +371,7 @@
         lines_low[place, :] = rest
 
     def line_step(step, carry):
-        l = col_at(step, -1)
+        l = col_far(step, -1)
 
         @pl.when(l < LINES)
         def _():
@@ -509,7 +514,7 @@
     lax.fori_loop(0, PAIRS // 11, column_products, 0)
 
     def columns_out(step_out, carry):
-        group = col_at(step_out, 1)
+        group = col_far(step_out, 1)
         place = pl.multiple_of(group * 8, 8)
         column = [None] * 64
         for step in range(PAIRS):
@@ -598,7 +603,7 @@
         lax.fori_loop(0, KEPT, send_term, 0)
 
     def line_out_step(step, carry):
-        l = col_at(step, 1)
+        l = col_far(step, 1)
 
         @pl.when(l < LINES)
         def _():

time: 144 us -> 145 us (level)
  no operation moved by 1% of the time
where the time goes in v3:
time: 145 us
  Pallas kernels  143 us (99%)
  local copies, waits for them, and re-layouts  2.26 us (2%)
    pallas_call x1, Pallas kernels, per_device(): pl.pallas_call(section_kernel, out_shape=jax.ShapeDtypeStruct(shape, FULL...  143 us

profile of v3, /device:TPU:1, one launch (start us, length us, event | category | flops | bytes accessed | tf_op | source)
XLA Modules:
  0.0 145.2 jit_solution(4011826228360581223)
XLA Ops:
  0.0 142.9 %section.1 = f32[2,256,512]{2,1,0:T(8,128)} custom-call(f32[2,256,512]{2,1,0:T(8,128)} %bitcast.7, f32[2,256,512]{2,1,0:T(8,128)} %bitcast.8, f32[2,256,512]{2,1,0:T(8,128)} %bitcast.9, f32[2,256,512]{2,1,0:T(8,128)} %bitcast.10, f32[2,256,512]{2,1,0:T(8,128)} %bitcast.11, bf16[2,128,96]{2,1,0:T(8,128)(2,1)} %constant.12.clone.first_table, ...), custom_call_target="tpu_custom_call" | custom-call | tf_op jit(solution)/shard_map/section/pallas_call | solution.py:654
  143.0 2.3 %copy.13 = f32[1,2,256,512]{3,2,1,0:T(8,128)} copy(f32[1,2,256,512]{3,2,1,0:T(8,128)} %bitcast.6) | data formatting | bytes 2097152

commit v4 on v2

--- a/solution.py
+++ b/solution.py
@@ -249,6 +249,11 @@
         along = lax.rem(lax.rem(col, 4) + 4 + sign * far_first(lax.rem(step, 4)), 4)
         return 4 * across + along
 
+    def col_far(step, sign):
+        across = lax.rem(col // 4 + 4 + sign * far_first(lax.rem(step, 4)), 4)
+        along = lax.rem(lax.rem(col, 4) + 4 + sign * far_first(step // 4), 4)
+        return 4 * across + along
+
     def row_at(step):
         across = lax.rem(row // 4 + far_first(step // 4), 4)
         return 4 * across + lax.bitwise_xor(lax.rem(row, 4), 3 - lax.rem(step, 4))
@@ -290,8 +295,8 @@
         lax.fori_loop(0, BLOCK_X // 8, shuffle, 0)
 
         def send(step, carry):
-            peer_row = row_at(lax.rem(step, ROWS))
-            peer_col = col_at(step // ROWS, 1)
+            peer_row = row_at(step // COLS)
+            peer_col = col_far(lax.rem(step, COLS), 1)
             line = peer_col * 8 + lax.rem(peer_row, 8) + 128 * (peer_row // 8)
             post(
                 sent_one.at[pl.ds(pl.multiple_of(line * 8, 8), 8)],

time: 144 us -> 148 us (1.028)
  Pallas kernels: 142 us -> 146 us
    pallas_call x1, Pallas kernels: 142 us -> 146 us  [per_device(): pl.pallas_call(section_kernel, out_shape=jax.ShapeDtypeStruct(shape, FULL...]
where the time goes in v4:
time: 148 us
  Pallas kernels  146 us (99%)
  local copies, waits for them, and re-layouts  2.26 us (2%)
    pallas_call x1, Pallas kernels, per_device(): pl.pallas_call(section_kernel, out_shape=jax.ShapeDtypeStruct(shape, FULL...  146 us

profile of v4, /device:TPU:1, one launch (start us, length us, event | category | flops | bytes accessed | tf_op | source)
XLA Modules:
  0.0 147.8 jit_solution(14802112648168263223)
XLA Ops:
  0.0 145.5 %section.1 = f32[2,256,512]{2,1,0:T(8,128)} custom-call(f32[2,256,512]{2,1,0:T(8,128)} %bitcast.7, f32[2,256,512]{2,1,0:T(8,128)} %bitcast.8, f32[2,256,512]{2,1,0:T(8,128)} %bitcast.9, f32[2,256,512]{2,1,0:T(8,128)} %bitcast.10, f32[2,256,512]{2,1,0:T(8,128)} %bitcast.11, bf16[2,128,96]{2,1,0:T(8,128)(2,1)} %constant.12.clone.first_table, ...), custom_call_target="tpu_custom_call" | custom-call | tf_op jit(solution)/shard_map/section/pallas_call | solution.py:654
  145.5 2.3 %copy.13 = f32[1,2,256,512]{3,2,1,0:T(8,128)} copy(f32[1,2,256,512]{3,2,1,0:T(8,128)} %bitcast.6) | data formatting | bytes 2097152
